TPU v7x, 16 devices: a 4x2x1 block of a 4x4x8 slice. The times are simulated.
16 devices in a mesh: rep: 2 (over y, z), dp: 8 (over x, core).
Axes of the slice: x: 4, y: 2, z: 1, core: 2. Of those that a mesh axis runs over, the one named last changes fastest.
The devices are a block of a 4x4x8 slice.
Arguments:
- x: bfloat16 [16, 2048, 1024], P(('rep', 'dp')), parts along dimension 0
- dy: bfloat16 [16, 2048, 1024], P(('rep', 'dp')), parts along dimension 0
- w_gate: bfloat16 [2, 1024, 3072], P(None, 'dp')
- w_up: bfloat16 [2, 1024, 3072], P(None, 'dp')
- w_down: bfloat16 [2, 3072, 1024], P(None, 'dp')
- m_w_gate: float32 [2, 1024, 3072], P(None, 'dp')
- m_w_up: float32 [2, 1024, 3072], P(None, 'dp')
- m_w_down: float32 [2, 3072, 1024], P(None, 'dp')
- v_w_gate: float32 [2, 1024, 3072], P(None, 'dp')
- v_w_up: float32 [2, 1024, 3072], P(None, 'dp')
- v_w_down: float32 [2, 3072, 1024], P(None, 'dp')
Outputs:
- output 1: bfloat16 [4, 1024, 3072], P('rep', 'dp'), parts along dimension 0
- output 2: bfloat16 [4, 1024, 3072], P('rep', 'dp'), parts along dimension 0
- output 3: bfloat16 [4, 3072, 1024], P('rep', 'dp'), parts along dimension 0
- output 4: float32 [4, 1024, 3072], P('rep', 'dp'), parts along dimension 0
- output 5: float32 [4, 1024, 3072], P('rep', 'dp'), parts along dimension 0
- output 6: float32 [4, 3072, 1024], P('rep', 'dp'), parts along dimension 0
- output 7: float32 [4, 1024, 3072], P('rep', 'dp'), parts along dimension 0
- output 8: float32 [4, 1024, 3072], P('rep', 'dp'), parts along dimension 0
- output 9: float32 [4, 3072, 1024], P('rep', 'dp'), parts along dimension 0
There are 2 independent parts. A program takes and returns all parts, laid end to end along the dimension named above; an argument that names none is the same for every part.
All inputs are finite; a program needn't handle non-finite values.
Results may differ from a plain program's by a relative error of at most 0.022.
Values are sent between devices in bfloat16 or wider.
A program may use at most 768 MiB of HBM per device.

v0:
```python
import jax
import jax.numpy as jnp
from jax import lax
from jax.sharding import PartitionSpec as P

NAMES = ("w_gate", "w_up", "w_down")


def matmul(a, w):
    return jnp.dot(a, w, preferred_element_type=jnp.float32).astype(jnp.bfloat16)


def normed(h):
    wide = h.astype(jnp.float32)
    scale = lax.rsqrt(jnp.mean(wide**2, -1, keepdims=True) + 1e-6)
    return (wide * scale).astype(jnp.bfloat16)


def layer(h, w):
    a = normed(h)
    gate = jnp.dot(a, w["w_gate"], preferred_element_type=jnp.float32)
    up = jnp.dot(a, w["w_up"], preferred_element_type=jnp.float32)
    return h + matmul((jax.nn.silu(gate) * up).astype(jnp.bfloat16), w["w_down"])


def adamw(w, m, v, g):
    m = 0.9 * m + 0.1 * g
    v = 0.95 * v + 0.05 * g * g
    step = m * lax.rsqrt(v + 1e-8) + 0.1 * w
    return (w - 0.02 * step).astype(jnp.bfloat16), m, v


def clipped(gradients, sum_of_squares, count):
    factor = jnp.minimum(1.0, 0.5 * lax.rsqrt(sum_of_squares / count + 1e-30))
    return [g * factor for g in gradients]


def solution(mesh):
    def fetched(weights, number):
        return {name: lax.all_gather(w[number], "dp", axis=0, tiled=True) for name, w in zip(NAMES, weights, strict=True)}

    def step(x, dy, *arrays):
        weights, m, v = (arrays[i : i + 3] for i in (0, 3, 6))
        layers = weights[0].shape[0]
        h, kept = x[0], []
        for number in range(layers):
            kept.append(h)
            h = layer(h, fetched(weights, number))
        by_h, mine = dy[0], [None] * layers
        for number in reversed(range(layers)):
            _, back = jax.vjp(lambda w, h: layer(h, w), fetched(weights, number), kept[number])
            by_w, by_h = back(by_h)
            mine[number] = [lax.psum_scatter(by_w[name], "dp", scatter_dimension=0, tiled=True) for name in NAMES]
        gradients = [jnp.stack([mine[number][i] for number in range(layers)]).astype(jnp.float32) for i in range(3)]
        squares = lax.psum(sum(jnp.sum(g * g) for g in gradients), "dp")
        gradients = clipped(gradients, squares, lax.psum(1, "dp") * sum(g.size for g in gradients))
        new = [adamw(w.astype(jnp.float32), m, v, g) for w, m, v, g in zip(weights, m, v, gradients, strict=True)]
        return tuple(one[which] for which in range(3) for one in new)

    states, cut = P(("rep", "dp"), None, None), P(None, "dp", None)
    return jax.shard_map(
        step,
        mesh=mesh,
        in_specs=(states, states) + (cut,) * 9,
        out_specs=(P("rep", "dp", None),) * 9,
        check_vma=False,
    )
```

profile of v0, /device:TPU:113, one launch (start us, length us, event | category | flops | bytes accessed | tf_op | source)
XLA Modules:
  0.0 632.2 jit_solution(17487433164328805801)
XLA Ops:
  32.3 17.7 %all-gather.13.cloned.1.call-done = bf16[1,1024,3072]{2,1,0:T(8,128)(2,1)} async-done(((bf16[1,128,3072]{2,1,0:T(8,128)(2,1)}), bf16[1,1024,3072]{2,1,0:T(8,128)(2,1)}) %all-gather.13.cloned.1.call-update) | async-done | bytes 6291472 | tf_op jit(solution)/shard_map/all_gather | solution.py:40
  50.0 20.0 %fusion.35 = f32[2048,3072]{1,0:T(8,128)} fusion(bf16[1,1024,3072]{2,1,0:T(8,128)(2,1)} %all-gather.13.cloned.1.call-done, bf16[1,2048,1024]{1,2,0:T(8,128)(2,1)} %copy.20, f32[2048]{0:T(1024)S(1)} %add_rsqrt_fusion), kind=kOutput, calls=%fused_computation.53 | convolution fusion | flops 12891193344 | bytes 35659776 | tf_op jit(solution)/shard_map/dot_general | solution.py:21
  70.0 18.8 %all-gather.15.cloned.1.call-done = bf16[1,1024,3072]{2,1,0:T(8,128)(2,1)} async-done(((bf16[1,128,3072]{2,1,0:T(8,128)(2,1)}), bf16[1,1024,3072]{2,1,0:T(8,128)(2,1)}) %all-gather.15.cloned.1.call-update) | async-done | bytes 6291472 | tf_op jit(solution)/shard_map/all_gather | solution.py:40
  88.9 33.5 %multiply_convert_fusion.1 = (bf16[2048,3072]{1,0:T(8,128)(2,1)}, f32[2048,3072]{1,0:T(8,128)}) fusion(f32[2048,3072]{1,0:T(8,128)} %fusion.35, bf16[1,1024,3072]{2,1,0:T(8,128)(2,1)} %all-gather.15.cloned.1.call-done, bf16[1,2048,1024]{1,2,0:T(8,128)(2,1)} %copy.20, f32[2048]{0:T(1024)S(1)} %add_rsqrt_fusion), kind=kOutput, calls=%fused_computation.17 | convolution fusion | flops 12928942080 | bytes 73408512 | tf_op jit(solution)/shard_map/dot_general | solution.py:22
  127.7 20.9 %fusion.19 = (f32[2048]{0:T(1024)S(1)}, bf16[2048,1024]{0,1:T(8,128)(2,1)}) fusion(bf16[2048,3072]{1,0:T(8,128)(2,1)} %get-tuple-element.24, bf16[1,3072,1024]{2,1,0:T(8,128)(2,1)} %all-gather.17.cloned.1.call-done, bf16[1,2048,1024]{1,2,0:T(8,128)(2,1)} %copy.20), kind=kOutput, calls=%fused_computation.37 | convolution fusion | flops 12895385600 | bytes 27271168 | tf_op jit(solution)/shard_map/dot_general | solution.py:10
  148.6 17.8 %all-gather.21.cloned.1.call-done = bf16[1,3072,1024]{2,1,0:T(8,128)(2,1)} async-done(((bf16[1,384,1024]{2,1,0:T(8,128)(2,1)}), bf16[1,3072,1024]{2,1,0:T(8,128)(2,1)}) %all-gather.21.cloned.1.call-update) | async-done | bytes 6291472 | tf_op jit(solution)/shard_map/all_gather | solution.py:40
  166.4 19.8 %convolution_convert_fusion.1 = bf16[2048,3072]{1,0:T(8,128)(2,1)} fusion(bf16[1,3072,1024]{2,1,0:T(8,128)(2,1)} %all-gather.21.cloned.1.call-done, bf16[1,2048,1024]{2,1,0:T(8,128)(2,1)} %param.12), kind=kOutput, calls=%fused_computation.29 | convolution fusion | flops 12891193344 | bytes 23068672 | tf_op jit(solution)/shard_map/transpose(jvp())/dot_general | solution.py:10
  186.3 18.8 %all-gather.23.cloned.1.call-done = bf16[1,1024,3072]{2,1,0:T(8,128)(2,1)} async-done(((bf16[1,128,3072]{2,1,0:T(8,128)(2,1)}), bf16[1,1024,3072]{2,1,0:T(8,128)(2,1)}) %all-gather.23.cloned.1.call-update) | async-done | bytes 6291472 | tf_op jit(solution)/shard_map/all_gather | solution.py:40
  205.1 19.9 %fusion.22 = f32[2048,3072]{1,0:T(8,128)} fusion(bf16[1,1024,3072]{2,1,0:T(8,128)(2,1)} %all-gather.23.cloned.1.call-done, bf16[2048,1024]{0,1:T(8,128)(2,1)} %get-tuple-element.27, f32[2048]{0:T(1024)S(1)} %fusion.80), kind=kOutput, calls=%fused_computation.40 | convolution fusion | flops 12891193344 | bytes 35659776 | tf_op jit(solution)/shard_map/jvp()/dot_general | solution.py:22
  225.0 18.8 %all-gather.19.cloned.1.call-done = bf16[1,1024,3072]{2,1,0:T(8,128)(2,1)} async-done(((bf16[1,128,3072]{2,1,0:T(8,128)(2,1)}), bf16[1,1024,3072]{2,1,0:T(8,128)(2,1)}) %all-gather.19.cloned.1.call-update) | async-done | bytes 6291472 | tf_op jit(solution)/shard_map/all_gather | solution.py:40
  243.8 37.2 %fusion.2 = (bf16[2048,3072]{1,0:T(8,128)(2,1)}, f32[2048,3072]{1,0:T(8,128)}) fusion(f32[2048,3072]{1,0:T(8,128)} %fusion.22, bf16[2048,3072]{1,0:T(8,128)(2,1)} %convolution_convert_fusion.1, bf16[1,1024,3072]{2,1,0:T(8,128)(2,1)} %all-gather.19.cloned.1.call-done, bf16[2048,1024]{0,1:T(8,128)(2,1)} %get-tuple-element.27, f32[2048]{0:T(1024)S(1)} %fusion.80), kind=kOutput, calls=%fused_computation.8 | convolution fusion | flops 12966690816 | bytes 85991424 | tf_op jit(solution)/shard_map/jvp()/dot_general | solution.py:21
  281.0 23.2 %fusion.12 = bf16[2048,1024]{0,1:T(8,128)(2,1)} fusion(bf16[2048,3072]{1,0:T(8,128)(2,1)} %convolution_convert_fusion.1, bf16[1,1024,3072]{2,1,0:T(8,128)(2,1)} %all-gather.23.cloned.1.call-done, f32[2048,3072]{1,0:T(8,128)} %get-tuple-element.29), kind=kOutput, calls=%fused_computation.21 | convolution fusion | flops 12922650624 | bytes 48234496 | tf_op jit(solution)/shard_map/transpose(jvp())/dot_general | solution.py:22
  304.2 20.9 %fusion.21 = (f32[2048]{0:T(1024)S(1)}, bf16[2048,1024]{0,1:T(8,128)(2,1)S(1)}) fusion(bf16[2048,1024]{0,1:T(8,128)(2,1)} %get-tuple-element.27, bf16[2048,1024]{0,1:T(8,128)(2,1)} %fusion.12, bf16[2048,3072]{1,0:T(8,128)(2,1)} %get-tuple-element.28, bf16[1,1024,3072]{2,1,0:T(8,128)(2,1)} %all-gather.19.cloned.1.call-done), kind=kOutput, calls=%fused_computation.39 | convolution fusion | flops 12895385600 | bytes 31465472 | tf_op jit(solution)/shard_map/transpose(jvp())/dot_general | solution.py:21
  330.4 17.2 %convolution_convert_fusion.3 = bf16[3072,1024]{1,0:T(8,128)(2,1)} fusion(bf16[2048,3072]{1,0:T(8,128)(2,1)} %get-tuple-element.24, bf16[2048,1024]{0,1:T(8,128)(2,1)S(1)} %fusion.44), kind=kOutput, calls=%fused_computation.60 | convolution fusion | flops 12888047616 | bytes 23068672 | tf_op jit(solution)/shard_map/transpose(jvp())/dot_general | solution.py:10
  347.7 25.7 %fusion.37 = bf16[3072,1024]{1,0:T(8,128)(2,1)} fusion(f32[2048,3072]{1,0:T(8,128)} %fusion.22, bf16[1,2048,1024]{2,1,0:T(8,128)(2,1)} %param.12, f32[2048,3072]{1,0:T(8,128)} %get-tuple-element.29), kind=kOutput, calls=%fused_computation.56 | convolution fusion | flops 12925796352 | bytes 60817408 | tf_op jit(solution)/shard_map/transpose(jvp())/dot_general | solution.py:10
  373.6 19.6 %convolution_convert_fusion = bf16[2048,3072]{1,0:T(8,128)(2,1)} fusion(bf16[2048,1024]{0,1:T(8,128)(2,1)} %copy-done.7, bf16[1,3072,1024]{2,1,0:T(8,128)(2,1)} %all-gather.17.cloned.1.call-done), kind=kOutput, calls=%fused_computation.28 | convolution fusion | flops 12891193344 | bytes 23068672 | tf_op jit(solution)/shard_map/transpose(jvp())/dot_general | solution.py:10
  393.2 20.9 %fusion.42 = bf16[1024,3072]{1,0:T(8,128)(2,1)} fusion(bf16[2048,3072]{1,0:T(8,128)(2,1)} %convolution_convert_fusion, f32[2048,3072]{1,0:T(8,128)} %fusion.35, bf16[1,2048,1024]{1,2,0:T(8,128)(2,1)S(1)} %copy-done.1, f32[2048]{0:T(1024)S(1)} %copy-done.21), kind=kOutput, calls=%fused_computation.59 | convolution fusion | flops 12932087808 | bytes 48242688 | tf_op jit(solution)/shard_map/transpose(jvp())/dot_general | solution.py:22
  414.7 22.1 %fusion.38 = bf16[1024,3072]{1,0:T(8,128)(2,1)} fusion(bf16[2048,3072]{1,0:T(8,128)(2,1)} %convolution_convert_fusion.1, bf16[2048,1024]{0,1:T(8,128)(2,1)} %get-tuple-element.27, f32[2048]{0:T(1024)S(1)} %copy-done.17, f32[2048,3072]{1,0:T(8,128)} %get-tuple-element.29), kind=kOutput, calls=%fused_computation.57 | convolution fusion | flops 12932087808 | bytes 48242688 | tf_op jit(solution)/shard_map/transpose(jvp())/dot_general | solution.py:22
  437.0 29.6 %fusion.39 = bf16[1024,3072]{1,0:T(8,128)(2,1)} fusion(f32[2048,3072]{1,0:T(8,128)} %fusion.35, f32[2048,3072]{1,0:T(8,128)} %get-tuple-element.25, bf16[2048,3072]{1,0:T(8,128)(2,1)} %convolution_convert_fusion, bf16[1,2048,1024]{1,2,0:T(8,128)(2,1)} %copy.20, f32[2048]{0:T(1024)S(1)} %copy-done.21), kind=kOutput, calls=%fused_computation.58 | convolution fusion | flops 12963545088 | bytes 73408512 | tf_op jit(solution)/shard_map/transpose(jvp())/dot_general | solution.py:21
  466.7 18.8 %convolution_convert_fusion.2 = bf16[1024,3072]{1,0:T(8,128)(2,1)} fusion(bf16[2048,3072]{1,0:T(8,128)(2,1)} %get-tuple-element.28, bf16[2048,1024]{0,1:T(8,128)(2,1)} %get-tuple-element.27, f32[2048]{0:T(1024)S(1)} %copy-done.17), kind=kOutput, calls=%fused_computation.55 | convolution fusion | flops 12891193344 | bytes 23076864 | tf_op jit(solution)/shard_map/transpose(jvp())/dot_general | solution.py:21
  488.5 18.3 %reduce-scatter.13.cloned.1.call-done = bf16[128,3072]{1,0:T(8,128)(2,1)} async-done(((bf16[1024,3072]{1,0:T(8,128)(2,1)}), bf16[128,3072]{1,0:T(8,128)(2,1)}) %reduce-scatter.13.cloned.1.call-update) | async-done | bytes 786448 | tf_op jit(solution)/shard_map/reduce_scatter | solution.py:53
  509.6 37.7 %reduce-scatter.7.cloned.1.call-done = bf16[128,3072]{1,0:T(8,128)(2,1)} async-done(((bf16[1024,3072]{1,0:T(8,128)(2,1)}), bf16[128,3072]{1,0:T(8,128)(2,1)}) %reduce-scatter.7.cloned.1.call-update) | async-done | bytes 786448 | tf_op jit(solution)/shard_map/reduce_scatter | solution.py:53
  547.3 40.3 %reduce-scatter.9.cloned.1.call-done = bf16[128,3072]{1,0:T(8,128)(2,1)} async-done(((bf16[1024,3072]{1,0:T(8,128)(2,1)}), bf16[128,3072]{1,0:T(8,128)(2,1)}) %reduce-scatter.9.cloned.1.call-update) | async-done | bytes 786448 | tf_op jit(solution)/shard_map/reduce_scatter | solution.py:53
  592.4 13.4 %psum.7 = f32[]{:T(128)} all-reduce(f32[]{:T(128)S(6)} %add.99), channel_id=1, replica_groups=mesh['rep'=2,'dp'=8] {'dp'}, use_global_device_ids=true, to_apply=%region_12.13 | all-reduce | flops 1 | bytes 8 | tf_op jit(solution)/shard_map/psum | solution.py:55
  (87 shorter events, 63.7 us)
Async XLA Ops:
  7.2 42.8 %all-gather.13.cloned.1.call-start = ((), (), s32[]{:S(2)}) async-start(), calls=%async_computation.12 | async-start | bytes 7077888 | tf_op jit(solution)/shard_map/all_gather | solution.py:40
  10.0 78.8 %all-gather.15.cloned.1.call-start = ((), (), s32[]{:S(2)}) async-start(), calls=%async_computation.13 | async-start | bytes 7077888 | tf_op jit(solution)/shard_map/all_gather | solution.py:40
  12.8 114.9 %all-gather.17.cloned.1.call-start = ((), (), s32[]{:S(2)}) async-start(), calls=%async_computation.14 | async-start | bytes 7077888 | tf_op jit(solution)/shard_map/all_gather | solution.py:40
  14.2 152.2 %all-gather.21.cloned.1.call-start = ((), (), s32[]{:S(2)}) async-start(), calls=%async_computation.16 | async-start | bytes 7077888 | tf_op jit(solution)/shard_map/all_gather | solution.py:40
  14.8 190.3 %all-gather.23.cloned.1.call-start = ((), (), s32[]{:S(2)}) async-start(), calls=%async_computation.17 | async-start | bytes 7077888 | tf_op jit(solution)/shard_map/all_gather | solution.py:40
  15.5 228.3 %all-gather.19.cloned.1.call-start = ((), (), s32[]{:S(2)}) async-start(), calls=%async_computation.15 | async-start | bytes 7077888 | tf_op jit(solution)/shard_map/all_gather | solution.py:40
  16.1 469.5 %reduce-scatter.15.cloned.1.call-start = ((), (), s32[]{:S(2)}) async-start(), calls=%async_computation.10 | async-start | bytes 7077888 | tf_op jit(solution)/shard_map/reduce_scatter | solution.py:53
  25.8 63.1 %copy-start.20 = (f32[2048]{0:T(1024)}, f32[2048]{0:T(1024)S(1)}, u32[]{:S(2)}) copy-start(f32[2048]{0:T(1024)S(1)} %add_rsqrt_fusion) | copy-start | bytes 24580
  148.6 37.7 %copy-start.18 = (f32[2048]{0:T(1024)}, f32[2048]{0:T(1024)S(1)}, u32[]{:S(2)}) copy-start(f32[2048]{0:T(1024)S(1)} %get-tuple-element.26) | copy-start | bytes 24580
  148.6 176.5 %copy-start.16 = (f32[2048]{0:T(1024)}, f32[2048]{0:T(1024)S(1)}, u32[]{:S(2)}) copy-start(f32[2048]{0:T(1024)S(1)} %fusion.80) | copy-start | bytes 24580
  304.2 20.9 %copy-start.19 = (f32[2048]{0:T(1024)S(1)}, f32[2048]{0:T(1024)}, u32[]{:S(2)}) copy-start(f32[2048]{0:T(1024)} %copy-done.18) | copy-start | bytes 24580
  304.2 20.9 %copy-start = (bf16[1,2048,1024]{1,2,0:T(8,128)(2,1)S(1)}, bf16[1,2048,1024]{1,2,0:T(8,128)(2,1)}, u32[]{:S(2)}) copy-start(bf16[1,2048,1024]{1,2,0:T(8,128)(2,1)} %copy.21) | copy-start | bytes 12582916
  304.2 20.9 %copy-start.6 = (bf16[2048,1024]{0,1:T(8,128)(2,1)S(1)}, bf16[2048,1024]{0,1:T(8,128)(2,1)}, u32[]{:S(2)}) copy-start(bf16[2048,1024]{0,1:T(8,128)(2,1)} %get-tuple-element.27) | copy-start | bytes 12582916
  347.6 138.0 %reduce-scatter.17.cloned.1.call-start = ((), (), s32[]{:S(2)}) async-start(), calls=%async_computation.11 | async-start | bytes 7077888 | tf_op jit(solution)/shard_map/reduce_scatter | solution.py:53
  373.5 19.7 %copy-start.21 = (f32[2048]{0:T(1024)S(1)}, f32[2048]{0:T(1024)}, u32[]{:S(2)}) copy-start(f32[2048]{0:T(1024)} %copy-done.20) | copy-start | bytes 24580
  373.5 115.1 %reduce-scatter.11.cloned.1.call-start = ((), (), s32[]{:S(2)}) async-start(), calls=%async_computation.8 | async-start | bytes 7077888 | tf_op jit(solution)/shard_map/reduce_scatter | solution.py:53
  373.5 19.6 %copy-start.1 = (bf16[1,2048,1024]{1,2,0:T(8,128)(2,1)S(1)}, bf16[1,2048,1024]{1,2,0:T(8,128)(2,1)}, u32[]{:S(2)}) copy-start(bf16[1,2048,1024]{1,2,0:T(8,128)(2,1)} %copy.20) | copy-start | bytes 12582916
  414.1 92.7 %reduce-scatter.13.cloned.1.call-start = ((), (), s32[]{:S(2)}) async-start(), calls=%async_computation.9 | async-start | bytes 7077888 | tf_op jit(solution)/shard_map/reduce_scatter | solution.py:53
  436.9 110.4 %reduce-scatter.7.cloned.1.call-start = ((), (), s32[]{:S(2)}) async-start(), calls=%async_computation.6 | async-start | bytes 7077888 | tf_op jit(solution)/shard_map/reduce_scatter | solution.py:53
  466.6 121.0 %reduce-scatter.9.cloned.1.call-start = ((), (), s32[]{:S(2)}) async-start(), calls=%async_computation.7 | async-start | bytes 7077888 | tf_op jit(solution)/shard_map/reduce_scatter | solution.py:53
  485.5 121.0 %copy-start.5 = (bf16[2,384,1024]{2,1,0:T(8,128)(2,1)S(1)}, bf16[2,384,1024]{2,1,0:T(8,128)(2,1)}, u32[]{:S(2)}) copy-start(bf16[2,384,1024]{2,1,0:T(8,128)(2,1)} %param.15) | copy-start | bytes 4718596
  587.6 26.2 %copy-start.14 = (bf16[128,3072]{1,0:T(8,128)(2,1)S(1)}, bf16[128,3072]{1,0:T(8,128)(2,1)}, u32[]{:S(2)}) copy-start(bf16[128,3072]{1,0:T(8,128)(2,1)} %reduce-scatter.7.cloned.1.call-done) | copy-start | bytes 2359300
  587.6 26.2 %copy-start.15 = (bf16[128,3072]{1,0:T(8,128)(2,1)S(1)}, bf16[128,3072]{1,0:T(8,128)(2,1)}, u32[]{:S(2)}) copy-start(bf16[128,3072]{1,0:T(8,128)(2,1)} %reduce-scatter.9.cloned.1.call-done) | copy-start | bytes 2359300
  606.7 10.9 %copy-start.13 = (bf16[128,3072]{1,0:T(8,128)(2,1)S(1)}, bf16[128,3072]{1,0:T(8,128)(2,1)}, u32[]{:S(2)}) copy-start(bf16[128,3072]{1,0:T(8,128)(2,1)} %reduce-scatter.13.cloned.1.call-done) | copy-start | bytes 2359300
  (10 other events, 69.9 us)
Sparse Core Ops, SparseCore 0:
  10.2 39.8 all-gather.12
  52.2 36.6 all-gather.14
  91.0 36.6 all-gather.16
  129.7 36.6 all-gather.20
  168.4 36.6 all-gather.22
  207.1 36.6 all-gather.18
  347.8 37.7 reduce-scatter.14
  387.8 38.1 reduce-scatter.16
  428.3 38.1 reduce-scatter.10
  468.6 38.1 reduce-scatter.12
  509.1 38.1 reduce-scatter.6
  549.4 38.1 reduce-scatter.8
where the time goes:
time: 643 us; the launch traced here: 632 us
  matrix products  349 us (54%)
  waiting for transfers between devices  196 us (30%)
  other arithmetic  29.5 us (5%)
  local copies, waits for them, and re-layouts  25.9 us (4%)
  between operations  17.6 us (3%)
  blocking collectives  13.4 us (2%)
    dot_general x5, matrix products, layer(): gate = jnp.dot(a, w['w_gate'], preferred_element_type=jnp.float32)  126 us
    dot_general x5, matrix products, layer(): up = jnp.dot(a, w['w_up'], preferred_element_type=jnp.float32)  120 us
    dot_general x5, matrix products, matmul(): jnp.dot(a, w, preferred_element_type=jnp.float32).astype(jnp.bfloat16)  103 us
    all_gather x6, waiting for transfers between devices, fetched(): lax.all_gather(w[number], 'dp', axis=0, tiled=True)  97.4 us
    reduce_scatter x6, waiting for transfers between devices, step(): lax.psum_scatter(by_w[name], 'dp', scatter_dimension=0, tiled=True)  96.3 us
    unnamed x46, local copies, waits for them, and re-layouts  19.3 us
    convert_element_type x2, other arithmetic, adamw(): return ((w - 0.02 * step).astype(jnp.bfloat16), m, v)  14.5 us
    psum x1, blocking collectives, step(): squares = lax.psum(sum((jnp.sum(g * g) for g in gradients)), 'dp')  13.4 us
  transfers between devices with their start and end apart: 12, of which 9 were waited for; matrix products, arithmetic and copies ran while one was open for 44% of the time, Pallas kernels for 0%

commit v1 on v0

v1 whole, which is shorter than its diff:
```python
import functools

import jax
import jax.numpy as jnp
from jax import lax
from jax.experimental import pallas as pl
from jax.experimental.pallas import tpu as pltpu
from jax.sharding import PartitionSpec as P

F32, BF16 = jnp.float32, jnp.bfloat16
MESH = pl.DeviceIdType.MESH
LANES = 128
TILE = 256
SLOTS = 6
NT = (((1,), (1,)), ((), ()))


def dot(a, b):
    return jnp.dot(a, b, preferred_element_type=F32)


def dot_nt(a, b):
    return lax.dot_general(a, b, NT, preferred_element_type=F32)


def loop(lo, hi, body):
    lax.fori_loop(lo, hi, lambda i, _: (body(i), None)[1], None)


def when(cond):
    return pl.when(cond)


def step_kernel(
    x_ref, dy_ref, wg_ref, wu_ref, wd_ref,
    gg_ref, gd_ref, ssq_ref, gu0_ref, p0_ref, h1_ref, a0t_ref, wd0_ref,
    a, at, dyb, dyt, acc, pbuf, gsl, wdr, dto, own, prt, st1, st2, r1, r2, gout, stg, sq, sqall,
    sem_in, sem_stg, sem_p, sem_h, sem_out, sem_own, sem_wd, sem_stash,
    ag_send, ag_recv, dg_send, dg_recv, r0_send, r0_recv, r1_send, r1_recv, r2_send, r2_recv, sq_send, sq_recv,
    *, n,
):
    chips = n // 2
    tokens, d = a.shape
    tiles = chips * 3
    mb, mf = tokens // 2, tokens // 4
    rb = tokens // 4
    me = lax.axis_index("dp")
    i, c = me // 2, me % 2
    ir, il, io = (i + 1) % chips, (i + chips - 1) % chips, (i + 2) % chips
    right, left, opp, partner = 2 * ir + c, 2 * il + c, 2 * io + c, 2 * i + (1 - c)

    def remote(src, dst, send, recv, to):
        return pltpu.make_async_remote_copy(src, dst, send, recv, device_id={"dp": to}, device_id_type=MESH)

    def in_copy(k, which):
        rows = pl.ds(k * rb, rb)
        return pltpu.make_async_copy((x_ref, dy_ref)[which].at[0, rows], (a, dyb)[which].at[rows], sem_in.at[which, k])

    for k in range(4):
        in_copy(k, 0).start()
        in_copy(k, 1).start()

    def has_gu(x):
        return ((x >= 0) & (x < tiles)) | ((x >= tiles + 4) & (x < 2 * tiles + 4))

    def gidx(x):
        return jnp.where(x < tiles, x, x - 4)

    def has_d(x):
        return (x >= 0) & (x < 2 * tiles)

    def gu_view(x, dev, half=None):
        s = lax.rem(gidx(x), SLOTS)
        if half is None:
            return gsl.at[s, dev]
        return gsl.at[s, dev, pl.ds(2 * half, 2)]

    def d_view(x, dev, half=None):
        s, k = lax.rem(x // 4, 3), lax.rem(x, 4)
        cols = pl.ds(pl.multiple_of(k * 256, 256), 256)
        if half is None:
            return wdr.at[s, dev, :, cols]
        return wdr.at[s, dev, pl.ds(64 * half, 64), cols]

    streams = (
        (has_gu, gu_view, ag_send, ag_recv, lambda x: lax.rem(gidx(x), SLOTS)),
        (has_d, d_view, dg_send, dg_recv, lambda x: lax.rem(x, SLOTS)),
    )

    def own_gu(x):
        g = gidx(x)
        layer, t = g // tiles, lax.rem(g, tiles)
        ch, q = t // 4, lax.rem(t, 4)
        s = lax.rem(g, SLOTS)
        out = []
        for b in range(4):
            col = pl.multiple_of(LANES * (6 * q + 3 * (b % 2) + ch), LANES)
            src = (wg_ref, wu_ref)[b // 2].at[layer, :, pl.ds(col, LANES)]
            out.append(pltpu.make_async_copy(src, gsl.at[s, me, b], sem_own.at[lax.rem(g, 2)]))
        return out

    def own_gu_wait(x):
        g = gidx(x)
        whole = gsl.at[lax.rem(g, SLOTS), me]
        pltpu.make_async_copy(whole, whole, sem_own.at[lax.rem(g, 2)]).wait()

    def own_d(chunk):
        layer, ch = chunk // 3, lax.rem(chunk, 3)
        return pltpu.make_async_copy(wd_ref.at[layer, pl.ds(pl.multiple_of(LANES * ch, LANES), LANES)], wdr.at[ch, me], sem_wd.at[ch])

    def stash(chunk):
        return pltpu.make_async_copy(wdr.at[chunk], wd0_ref.at[chunk], sem_stash)

    def ag_copies(view, send, recv, s, x):
        def cp(name_s, name_r, dev, to, half=None):
            v = view(x, dev, half)
            return remote(v, v, send.at[name_s, s], recv.at[name_r, s], to)
        return dict(
            own_r=lambda: cp(0, 0, me, right), own_l=lambda: cp(1, 1, me, left), own_p=lambda: cp(2, 2, me, partner),
            l_p=lambda: cp(3, 3, left, partner), l_r=lambda: cp(4, 4, left, right, 0),
            r_p=lambda: cp(5, 5, right, partner), r_l=lambda: cp(6, 6, right, left, 1),
            o_p=lambda: cp(7, 7, opp, partner),
        )

    def got(view, recv, send, s, x, name, dev, half=None):
        v = view(x, dev, half)
        remote(v, v, send.at[name, s], recv.at[name, s], partner).wait_recv()

    def other(dev):
        return dev + 1 - 2 * lax.rem(dev, 2)

    def ag_step(t):
        @when(has_gu(t + 4))
        def _():
            for cp in own_gu(t + 4):
                cp.start()

        x4 = t + 4
        @when(has_d(x4) & (lax.rem(x4, 4) == 0) & (x4 >= tiles))
        def _():
            own_d(x4 // 4).start()

        for has, view, send, recv, sl in streams:
            x = t + 3
            @when(has(x))
            def _():
                if view is gu_view:
                    own_gu_wait(x)
                else:
                    @when(lax.rem(x, 4) == 0)
                    def _():
                        own_d(x // 4).wait()
                k = ag_copies(view, send, recv, sl(x), x)
                k["own_r"]().start()
                k["own_l"]().start()
                k["own_p"]().start()
        for has, view, send, recv, sl in streams:
            y = t + 2
            @when(has(y))
            def _():
                s = sl(y)
                k = ag_copies(view, send, recv, s, y)
                got(view, recv, send, s, y, 0, left)
                k["l_r"]().start()
                k["l_p"]().start()
                got(view, recv, send, s, y, 1, right)
                k["r_l"]().start()
                k["r_p"]().start()
        for has, view, send, recv, sl in streams:
            z = t + 1
            @when(has(z))
            def _():
                s = sl(z)
                got(view, recv, send, s, z, 4, opp, 0)
                got(view, recv, send, s, z, 6, opp, 1)
                ag_copies(view, send, recv, s, z)["o_p"]().start()
        for has, view, send, recv, sl in streams:
            @when(has(t))
            def _():
                s = sl(t)
                got(view, recv, send, s, t, 2, partner)
                got(view, recv, send, s, t, 3, other(left))
                got(view, recv, send, s, t, 5, other(right))
                got(view, recv, send, s, t, 7, other(opp))
                for make in ag_copies(view, send, recv, s, t).values():
                    make().wait_send()

    steps = 2 * tiles + 4
    half_d, full_d, full_gu = LANES, 2 * LANES, 4 * LANES

    def has_rs_gu(r):
        return ((r >= 0) & (r < tiles)) | ((r >= tiles + 4) & (r < steps))

    def has_rs_d(r):
        return (r >= 4) & (r < steps)

    parts = ((has_rs_gu, 0, 0, full_gu), (has_rs_d, 1, full_gu, full_d))

    def total(r, j, rows):
        return own[lax.rem(r, 4), c, j, rows].astype(F32) + prt[lax.rem(r, 5), j, rows].astype(F32)

    def blocks(lo, first, count, body):
        loop(first, first + count, lambda b: body(pl.ds(pl.multiple_of(lo + b * LANES, LANES), LANES)))

    def rs_cores(part, r):
        _, w, lo, size = part
        s = lax.rem(r, 5)
        rows = pl.ds(lo, size)
        return remote(own.at[lax.rem(r, 4), 1 - c, :, rows], prt.at[s, :, rows], r0_send.at[w, s], r0_recv.at[w, s], partner)

    def rs_far(part, r, side):
        _, w, lo, size = part
        s = lax.rem(r, 2)
        rows = pl.ds(lo + side * (size // 2), size // 2)
        return remote(st1.at[s, rows], r1.at[s, rows], r1_send.at[w, side, s], r1_recv.at[w, side, s], (right, left)[side])

    def rs_near(part, r, side):
        _, w, lo, size = part
        s = lax.rem(r, 4)
        rows = pl.ds(lo, size)
        return remote(st2.at[lax.rem(r, 2), side, rows], r2.at[s, side, rows], r2_send.at[w, side, s], r2_recv.at[w, side, s], (right, left)[side])

    def out_copy(part, r):
        _, w, lo, size = part
        s = lax.rem(r, 2)
        to = gg_ref.at[jnp.where(r < tiles, r, r - 4)] if w == 0 else gd_ref.at[r - 4]
        return pltpu.make_async_copy(gout.at[s, pl.ds(lo, size)], to, sem_out.at[w, s])

    def rs_serve(t):
        for part in parts:
            has, w, lo, size = part
            r = t - 4
            @when(has(r))
            def _():
                s, s2 = lax.rem(r, 4), lax.rem(r, 2)
                rs_near(part, r, 0).wait()
                rs_near(part, r, 1).wait()
                @when(r >= 4 * w + 2)
                def _():
                    out_copy(part, r).wait()
                def body(rows):
                    g = total(r, i, rows) + r2[s, 0, rows].astype(F32) + r2[s, 1, rows].astype(F32)
                    g = g.astype(BF16)
                    gout[s2, rows] = g
                    g = g.astype(F32)
                    sq[...] += jnp.sum((g * g).reshape(LANES // 8, 8, LANES), axis=0)
                blocks(lo, 0, size // LANES, body)
                out_copy(part, r).start()
        for part in parts:
            has, _, lo, size = part
            r = t - 2
            @when(has(r))
            def _():
                s2 = lax.rem(r, 2)
                rs_far(part, r, 0).wait()
                rs_far(part, r, 1).wait()
                half = size // 2 // LANES
                for side, j in ((0, ir), (1, il)):
                    def with_more(rows):
                        st2[s2, side, rows] = (total(r, j, rows) + r1[s2, rows].astype(F32)).astype(BF16)
                    def without(rows):
                        st2[s2, side, rows] = total(r, j, rows).astype(BF16)
                    blocks(lo, side * half, half, with_more)
                    blocks(lo, half - side * half, half, without)
                    rs_near(part, r, side).start()
        for part in parts:
            has, _, lo, size = part
            r = t - 1
            @when(has(r))
            def _():
                s2 = lax.rem(r, 2)
                rs_cores(part, r).wait()
                def body(rows):
                    st1[s2, rows] = total(r, io, rows).astype(BF16)
                blocks(lo, 0, size // LANES, body)
                rs_far(part, r, 0).start()
                rs_far(part, r, 1).start()

    def rs_begin(r):
        @when(has_rs_gu(r))
        def _():
            rs_cores(parts[0], r).start()
        @when(has_rs_d(r))
        def _():
            @when(r < tiles + 4)
            def _():
                s, k = lax.rem(r, 4), lax.rem(r, 4)
                cs = lax.rem(r // 4 - 1, 2)
                def body(dev):
                    cc, j = dev // chips, lax.rem(dev, chips)
                    own[s, cc, j, pl.ds(full_gu, full_d)] = dto[cs, cc, j, pl.ds(pl.multiple_of(k * full_d, full_d), full_d)]
                loop(0, n, body)
            rs_cores(parts[1], r).start()

    def back(g, u, dp):
        sig = 0.5 * jnp.tanh(0.5 * g) + 0.5
        silu = g * sig
        dp = dp.astype(BF16).astype(F32)
        return silu, (dp * u * (sig * (1 + g * (1 - sig)))).astype(BF16), (dp * silu).astype(BF16)

    def gate_up(s):
        return jnp.concatenate([gsl[s, :, b].reshape(d, LANES) for b in range(4)], axis=1)

    def down_tile(s, q):
        return wdr[s, pl.ds(2 * q, 2)].reshape(TILE, d)

    def gate_up_grads(r):
        s, m = lax.rem(r, 4), d // 2
        def body(k):
            val = dot(at[pl.ds(pl.multiple_of(k * m, m), m)], pbuf[:, TILE : 3 * TILE]).astype(BF16)
            for e in range(m // TILE):
                for cc in range(2):
                    lo = TILE * e + LANES * cc
                    for b in range(4):
                        own[s, cc, 2 * k + e, LANES * b : LANES * b + LANES] = val[lo : lo + LANES, LANES * b : LANES * b + LANES]
        loop(0, 2, body)

    def down_grads_one(t):
        cs, q, m = lax.rem(t // 4, 2), lax.rem(t, 4), d // 2
        def body(k):
            rows = pl.ds(pl.multiple_of(k * m, m), m)
            val = dot(dyt[rows], pbuf[:, :TILE]).astype(BF16)
            for cc in range(2):
                dto[cs, cc, q, rows] = val[:, LANES * cc : LANES * cc + LANES]
        loop(0, 2, body)

    def down_grads_zero(t, r):
        s = lax.rem(r, 4)
        val = dot(dyt[pl.ds(pl.multiple_of(lax.rem(t, 4) * TILE, TILE), TILE)], a[...]).astype(BF16)
        for dev in range(n):
            own[s, dev % 2, dev // 2, full_gu:] = val[:, LANES * dev : LANES * dev + LANES]

    def norm_rows(h):
        wide = h.astype(F32)
        scale = lax.rsqrt(jnp.mean(wide * wide, -1, keepdims=True) + 1e-6)
        return (wide * scale).astype(BF16)

    barrier = pltpu.get_barrier_semaphore()
    for k in range(1, n):
        pl.semaphore_signal(barrier, inc=1, device_id={"dp": lax.rem(me + k, n)}, device_id_type=MESH)
    for k in range(3):
        own_d(k).start()
    sq[...] = jnp.zeros_like(sq)
    pl.semaphore_wait(barrier, n - 1)

    def prologue(k):
        ag_step(k - 4)
        in_copy(k, 0).wait()
        in_copy(k, 1).wait()
        rows = pl.ds(pl.multiple_of(k * rb, rb), rb)
        av = norm_rows(a[rows])
        a[rows] = av
        at[:, rows] = av.T
        dyt[:, rows] = dyb[rows].T
        acc[rows] = jnp.zeros_like(acc[rows])
    loop(0, 4, prologue)
    a0t_copy = pltpu.make_async_copy(at, a0t_ref, sem_h.at[0])
    a0t_copy.start()

    def stg_copy(t, m):
        return pltpu.make_async_copy(stg, gu0_ref.at[t, :, pl.ds(pl.multiple_of(m * mf, mf), mf)], sem_stg)

    def p_copy(t):
        q = lax.rem(t, 4)
        cols = pl.ds(pl.multiple_of(q * TILE, TILE), TILE)
        return pltpu.make_async_copy(pbuf.at[:, cols], p0_ref.at[t // 4, :, cols], sem_p.at[q])

    def forward(t):
        ag_step(t)
        q, ch = lax.rem(t, 4), t // 4
        s = lax.rem(t, SLOTS)
        @when((q == 1) & (t > 4))
        def _():
            stash((t - 5) // 4).wait()
        @when(t >= 4)
        def _():
            p_copy(t).wait()
        def rows_of(m):
            rows = pl.ds(pl.multiple_of(m * mf, mf), mf)
            val = dot(a[rows], gate_up(s))
            g, u = val[:, :TILE], val[:, TILE:]
            @when((m > 0) | (t > 0))
            def _():
                stg_copy(t, m).wait()
            stg[0] = g
            stg[1] = u
            stg_copy(t, m).start()
            sig = 0.5 * jnp.tanh(0.5 * g) + 0.5
            pbuf[rows, pl.ds(pl.multiple_of(q * TILE, TILE), TILE)] = (g * sig * u).astype(BF16)
        loop(0, tokens // mf, rows_of)
        p_copy(t).start()
        @when(q == 3)
        def _():
            stash(ch).start()
            def down(m):
                rows = pl.ds(pl.multiple_of(m * mf, mf), mf)
                acc[rows] += dot(pbuf[rows], wdr[ch].reshape(d, d))
            loop(0, tokens // mf, down)
    loop(0, tiles, forward)
    stg_copy(0, 0).wait()
    for q in range(4):
        p_copy(q).wait()
    a0t_copy.wait()

    def x_again(k):
        rows = pl.ds(pl.multiple_of(k * rb, rb), rb)
        return pltpu.make_async_copy(x_ref.at[0, rows], pbuf.at[rows], sem_in.at[0, k])

    def h_out(k):
        rows = pl.ds(pl.multiple_of(k * rb, rb), rb)
        return pltpu.make_async_copy(pbuf.at[rows], h1_ref.at[rows], sem_in.at[1, k])

    for k in range(4):
        x_again(k).start()

    def between(k):
        ag_step(tiles + k)
        @when(k == 1)
        def _():
            stash(2).wait()
        x_again(k).wait()
        rows = pl.ds(pl.multiple_of(k * rb, rb), rb)
        h = (pbuf[rows].astype(F32) + acc[rows].astype(BF16).astype(F32)).astype(BF16)
        pbuf[rows] = h
        h_out(k).start()
        av = norm_rows(h)
        a[rows] = av
        at[:, rows] = av.T
        acc[rows] = jnp.zeros_like(acc[rows])
    loop(0, 4, between)
    for k in range(4):
        h_out(k).wait()

    def layer_one(t):
        ag_step(tiles + 4 + t)
        q, ch = lax.rem(t, 4), t // 4
        s = lax.rem(tiles + t, SLOTS)
        def rows_of(m):
            rows = pl.ds(pl.multiple_of(m * mb, mb), mb)
            val = dot(a[rows], gate_up(s))
            g, u = val[:, :TILE], val[:, TILE:]
            dp = dot_nt(dyb[rows], down_tile(ch, q))
            silu, dg, du = back(g, u, dp)
            pbuf[rows, :TILE] = (silu * u).astype(BF16)
            pbuf[rows, TILE : 2 * TILE] = dg
            pbuf[rows, 2 * TILE : 3 * TILE] = du
            acc[rows] += dot_nt(jnp.concatenate([dg, du], axis=1), gate_up(s))
        loop(0, tokens // mb, rows_of)
        rs_serve(t)
        gate_up_grads(t)
        down_grads_one(t)
        rs_begin(t)
    loop(0, tiles, layer_one)

    def h_in(k):
        rows = pl.ds(pl.multiple_of(k * rb, rb), rb)
        return pltpu.make_async_copy(h1_ref.at[rows], pbuf.at[rows], sem_in.at[1, k])

    for k in range(4):
        h_in(k).start()
    a0t_in = pltpu.make_async_copy(a0t_ref, at, sem_h.at[0])
    a0t_in.start()
    wd0_in = pltpu.make_async_copy(wd0_ref, wdr, sem_stash)
    wd0_in.start()

    def turn(k):
        rs_serve(tiles + k)
        rs_begin(tiles + k)
        h_in(k).wait()
        def part(e):
            rows = pl.ds(pl.multiple_of(k * rb + e * LANES, LANES), LANES)
            da = acc[rows].astype(BF16).astype(F32)
            wide = pbuf[rows].astype(F32)
            scale = lax.rsqrt(jnp.mean(wide * wide, -1, keepdims=True) + 1e-6)
            by_scale = jnp.sum(da * wide, -1, keepdims=True)
            by_h = (da * scale - wide * (scale * scale * scale * by_scale * (1 / d))).astype(BF16)
            dyb[rows] = (dyb[rows].astype(F32) + by_h.astype(F32)).astype(BF16)
        loop(0, rb // LANES, part)
        rows = pl.ds(pl.multiple_of(k * rb, rb), rb)
        dyt[:, rows] = dyb[rows].T
    loop(0, 4, turn)

    def gu_in(t, which):
        s = lax.rem(t, 2)
        cols = pl.ds(pl.multiple_of(2 * TILE * s + TILE * which, TILE), TILE)
        return pltpu.make_async_copy(gu0_ref.at[t, which], acc.at[:, cols], sem_h.at[1 + which + 2 * s])

    def p_in(ch):
        return pltpu.make_async_copy(p0_ref.at[ch], a, sem_p.at[0])

    gu_in(0, 0).start()
    gu_in(0, 1).start()
    a0t_in.wait()
    wd0_in.wait()

    def layer_zero(t):
        q, ch = lax.rem(t, 4), t // 4
        @when(q == 0)
        def _():
            p_in(ch).start()
        @when(t + 1 < tiles)
        def _():
            gu_in(t + 1, 0).start()
            gu_in(t + 1, 1).start()
        gu_in(t, 0).wait()
        gu_in(t, 1).wait()
        base = pl.multiple_of(2 * TILE * lax.rem(t, 2), 2 * TILE)
        def rows_of(m):
            rows = pl.ds(pl.multiple_of(m * mb, mb), mb)
            dp = dot_nt(dyb[rows], down_tile(ch, q))
            g = acc[rows, pl.ds(base, TILE)]
            u = acc[rows, pl.ds(pl.multiple_of(base + TILE, TILE), TILE)]
            _, dg, du = back(g, u, dp)
            pbuf[rows, TILE : 2 * TILE] = dg
            pbuf[rows, 2 * TILE : 3 * TILE] = du
        loop(0, tokens // mb, rows_of)
        r = tiles + 4 + t
        rs_serve(r)
        @when(q == 0)
        def _():
            p_in(ch).wait()
        gate_up_grads(r)
        down_grads_zero(t, r)
        rs_begin(r)
    loop(0, tiles, layer_zero)
    loop(steps, steps + 4, rs_serve)
    for part in parts:
        out_copy(part, steps - 2).wait()
        out_copy(part, steps - 1).wait()

    def sq_copy(k):
        return remote(sq, sqall.at[k - 1], sq_send.at[k - 1], sq_recv.at[k - 1], lax.rem(me + k, n))
    for k in range(1, n):
        sq_copy(k).start()
    for k in range(1, n):
        sq_copy(k).wait()
    ssq_ref[...] = sq[...] + jnp.sum(sqall[...], axis=0)


def run_step(x, dy, wg, wu, wd, n):
    _, tokens, d = x.shape
    layers, rows, ff = wg.shape
    tiles = ff // TILE
    any_ = pl.BlockSpec(memory_space=pl.ANY)
    dma = pltpu.SemaphoreType.DMA
    v = pltpu.VMEM
    matmul = 2 * tokens * d * ff
    return pl.pallas_call(
        functools.partial(step_kernel, n=n),
        out_shape=(
            jax.ShapeDtypeStruct((2 * tiles, 512, LANES), BF16),
            jax.ShapeDtypeStruct((2 * tiles, 256, LANES), BF16),
            jax.ShapeDtypeStruct((8, LANES), F32),
            jax.ShapeDtypeStruct((tiles, 2, tokens, TILE), F32),
            jax.ShapeDtypeStruct((3, tokens, tiles // 3 * TILE), BF16),
            jax.ShapeDtypeStruct((tokens, d), BF16),
            jax.ShapeDtypeStruct((d, tokens), BF16),
            jax.ShapeDtypeStruct((3, n, LANES, d), BF16),
        ),
        in_specs=[any_] * 5,
        out_specs=(any_, any_, pl.BlockSpec(memory_space=pltpu.VMEM), any_, any_, any_, any_, any_),
        scratch_shapes=[
            v((tokens, d), BF16), v((d, tokens), BF16), v((tokens, d), BF16), v((d, tokens), BF16),
            v((tokens, d), F32), v((tokens, d), BF16),
            v((SLOTS, n, 4, LANES, LANES), BF16), v((3, n, LANES, d), BF16),
            v((2, 2, n // 2, d, LANES), BF16), v((4, 2, n // 2, 768, LANES), BF16), v((5, n // 2, 768, LANES), BF16),
            v((2, 768, LANES), BF16), v((2, 2, 768, LANES), BF16), v((2, 768, LANES), BF16), v((4, 2, 768, LANES), BF16),
            v((2, 768, LANES), BF16), v((2, tokens // 4, TILE), F32), v((8, LANES), F32), v((n - 1, 8, LANES), F32),
            dma((2, 4)), dma(()), dma((4,)), dma((5,)), dma((2, 2)), dma((2,)), dma((3,)), dma(()),
            dma((8, SLOTS)), dma((8, SLOTS)), dma((8, SLOTS)), dma((8, SLOTS)),
            dma((2, 5)), dma((2, 5)), dma((2, 2, 2)), dma((2, 2, 2)), dma((2, 2, 4)), dma((2, 2, 4)), dma((n - 1,)), dma((n - 1,)),
        ],
        compiler_params=pltpu.CompilerParams(collective_id=0, has_side_effects=True, vmem_limit_bytes=67_000_000),
        cost_estimate=pl.CostEstimate(flops=15 * matmul, bytes_accessed=200_000_000, transcendentals=2 * tokens * ff),
        name="step",
    )(x, dy, wg, wu, wd)


def adamw_kernel(count, ssq_ref, gg_ref, gd_ref, *refs):
    ins, outs = refs[:9], refs[9:]
    mean = jnp.sum(ssq_ref[...]) / count
    factor = jnp.minimum(1.0, 0.5 * lax.rsqrt(jnp.full((8, LANES), mean, F32) + 1e-30))[0:1, 0:1]

    def update(which, rows, cols, g):
        at = (0, rows, cols)
        g = g.astype(F32) * factor
        w, m, v = (ins[3 * k + which][at] for k in range(3))
        m = 0.9 * m + 0.1 * g
        v = 0.95 * v + 0.05 * g * g
        w = w.astype(F32)
        outs[which][at] = (w - 0.02 * (m * lax.rsqrt(v + 1e-8) + 0.1 * w)).astype(BF16)
        outs[3 + which][at] = m
        outs[6 + which][at] = v

    every = slice(None)
    tiles = gg_ref.shape[0]
    for t in range(tiles):
        for b in range(4):
            col = LANES * (6 * (t % 4) + 3 * (b % 2) + t // 4)
            update(b // 2, every, slice(col, col + LANES), gg_ref[t, b])
    for ch in range(3):
        update(2, slice(LANES * ch, LANES * ch + LANES), every, gd_ref[0, ch, 0].astype(F32).T)


def run_adamw(count, ssq, gg, gd, arrays):
    layers, rows, ff = arrays[0].shape
    _, drows, d = arrays[2].shape
    tiles = ff // TILE
    parts = 4
    gg = gg.reshape(layers * tiles, 4, LANES, LANES)
    gd = gd.reshape(layers, 3, 4, 256, LANES)
    wide = pl.BlockSpec((1, rows // parts, ff), lambda l, p: (l, p, 0))
    tall = pl.BlockSpec((1, drows, d // parts), lambda l, p: (l, 0, p))
    specs = [wide, wide, tall]
    last = layers - 1
    return pl.pallas_call(
        functools.partial(adamw_kernel, count),
        grid=(layers, parts),
        out_shape=tuple(jax.ShapeDtypeStruct(a.shape, a.dtype) for a in arrays),
        in_specs=[
            pl.BlockSpec((8, LANES), lambda l, p: (0, 0)),
            pl.BlockSpec((tiles, 4, rows // parts, LANES), lambda l, p: (last - l, 0, p, 0)),
            pl.BlockSpec((1, 3, 1, 256, LANES), lambda l, p: (last - l, 0, p, 0, 0)),
        ] + specs * 3,
        out_specs=tuple(specs * 3),
        compiler_params=pltpu.CompilerParams(vmem_limit_bytes=60_000_000),
        name="adamw",
    )(ssq, gg, gd, *arrays)


def solution(mesh):
    n = mesh.shape["dp"]

    def step(x, dy, *arrays):
        gg, gd, ssq = run_step(x, dy, *arrays[:3], n)[:3]
        count = float(n * sum(w.size for w in arrays[:3]))
        return run_adamw(count, ssq, gg, gd, arrays)

    states, cut = P(("rep", "dp"), None, None), P(None, "dp", None)
    return jax.shard_map(
        step,
        mesh=mesh,
        in_specs=(states, states) + (cut,) * 9,
        out_specs=(P("rep", "dp", None),) * 9,
        check_vma=False,
    )
```

time: 643 us -> 439 us (0.68); the launches traced: 632 us -> 439 us
  Pallas kernels: 0 us -> 438 us
  matrix products: 349 us -> 0 us
  waiting for transfers between devices: 196 us -> 0 us
  other arithmetic: 29.5 us -> 0 us
  local copies, waits for them, and re-layouts: 25.9 us -> 0 us
  between operations: 17.6 us -> 0.81 us
  blocking collectives: 13.4 us -> 0 us
    pallas_call x0 -> x2, Pallas kernels: none -> 438 us  [the longest x1 420 us: run_step(): pl.pallas_call(functools.partial(step_kernel, n=n), out_shape=(jax.ShapeD...]
    dot_general x15 -> x0, matrix products: 349 us -> none  [the longest x5 126 us: layer(): gate = jnp.dot(a, w['w_gate'], preferred_element_type=jnp.float32)]
    all_gather x6 -> x0, waiting for transfers between devices: 97.4 us -> none  [fetched(): lax.all_gather(w[number], 'dp', axis=0, tiled=True)]
    reduce_scatter x6 -> x0, waiting for transfers between devices: 96.3 us -> none  [step(): lax.psum_scatter(by_w[name], 'dp', scatter_dimension=0, tiled=True)]
    unnamed x46 -> x0, local copies, waits for them, and re-layouts: 19.3 us -> none
    convert_element_type x2 -> x0, other arithmetic: 14.5 us -> none  [adamw(): return ((w - 0.02 * step).astype(jnp.bfloat16), m, v)]
    psum x1 -> x0, blocking collectives: 13.4 us -> none  [step(): squares = lax.psum(sum((jnp.sum(g * g) for g in gradients)), 'dp')]
    reduce_sum x4 -> x0, other arithmetic: 11.6 us -> none  [the longest x3 8.57 us: step(): squares = lax.psum(sum((jnp.sum(g * g) for g in gradients)), 'dp')]
  transfers between devices with their start and end apart: 12 -> 0, of which waited for: 9 -> 0; matrix products, arithmetic and copies ran while one was open for 44% -> 0% of each run, Pallas kernels for 0% -> 0%
where the time goes in v1:
time: 439 us
  Pallas kernels  438 us (100%)
    pallas_call x1, Pallas kernels, run_step(): pl.pallas_call(functools.partial(step_kernel, n=n), out_shape=(jax.ShapeD...  420 us
    pallas_call x1, Pallas kernels, run_adamw(): pl.pallas_call(functools.partial(adamw_kernel, count), grid=(layers, part...  18.2 us

profile of v1, /device:TPU:113, one launch (start us, length us, event | category | flops | bytes accessed | tf_op | source)
XLA Modules:
  0.0 438.8 jit_solution(7008232733357673075)
XLA Ops:
  0.6 419.8 %step.1 = (bf16[24,512,128]{2,1,0:T(8,128)(2,1)}, bf16[24,256,128]{2,1,0:T(8,128)(2,1)}, f32[8,128]{1,0:T(8,128)}, f32[12,2,2048,256]{3,2,1,0:T(8,128)}, bf16[3,...) custom-call(bf16[1,2048,1024]{2,1,0:T(8,128)(2,1)} %x_ref.1, ...), custom_call_target="tpu_custom_call" | custom-call | flops 193273528320 | bytes 200000000 | tf_op jit(solution)/shard_map/step/pallas_call | solution.py:548
  420.4 18.2 %adamw.1 = (bf16[2,128,3072]{2,1,0:T(8,128)(2,1)}, bf16[2,128,3072]{2,1,0:T(8,128)(2,1)}, bf16[2,384,1024]{2,1,0:T(8,128)(2,1)}, f32[2,128,3072]{2,1,0:T(8,128)}...) custom-call(f32[8,128]{1,0:T(8,128)} %get-tuple-element.12.ssq_ref, ...), custom_call_target="tpu_custom_call" | custom-call | tf_op jit(solution)/shard_map/adamw/pallas_call | solution.py:616

commit v2 on v1

--- a/solution.py
+++ b/solution.py
@@ -11,7 +11,7 @@
 MESH = pl.DeviceIdType.MESH
 LANES = 128
 TILE = 256
-SLOTS = 6
+SLOTS = 7
 NT = (((1,), (1,)), ((), ()))
 
 
@@ -34,7 +34,7 @@
 def step_kernel(
     x_ref, dy_ref, wg_ref, wu_ref, wd_ref,
     gg_ref, gd_ref, ssq_ref, gu0_ref, p0_ref, h1_ref, a0t_ref, wd0_ref,
-    a, at, dyb, dyt, acc, pbuf, gsl, wdr, dto, own, prt, st1, st2, r1, r2, gout, stg, sq, sqall,
+    a, at, dyb, dyt, acc, pbuf, gsl, wdr, dto, own, prt, st2, r1, r2, gout, stg, sq, sqall,
     sem_in, sem_stg, sem_p, sem_h, sem_out, sem_own, sem_wd, sem_stash,
     ag_send, ag_recv, dg_send, dg_recv, r0_send, r0_recv, r1_send, r1_recv, r2_send, r2_recv, sq_send, sq_recv,
     *, n,
@@ -42,15 +42,20 @@
     chips = n // 2
     tokens, d = a.shape
     tiles = chips * 3
-    mb, mf = tokens // 2, tokens // 4
+    mb, mf = tokens // 2, tokens // 2
     rb = tokens // 4
     me = lax.axis_index("dp")
     i, c = me // 2, me % 2
     ir, il, io = (i + 1) % chips, (i + chips - 1) % chips, (i + 2) % chips
     right, left, opp, partner = 2 * ir + c, 2 * il + c, 2 * io + c, 2 * i + (1 - c)
+    group = lax.axis_index("rep")
+    h = lax.rem(group, 2)
+    peer = {"rep": group + 1 - 2 * h}
+    strong, weak = jnp.where(h == 0, left, right), jnp.where(h == 0, right, left)
 
     def remote(src, dst, send, recv, to):
-        return pltpu.make_async_remote_copy(src, dst, send, recv, device_id={"dp": to}, device_id_type=MESH)
+        to = to if isinstance(to, dict) else {"dp": to}
+        return pltpu.make_async_remote_copy(src, dst, send, recv, device_id=to, device_id_type=MESH)
 
     def in_copy(k, which):
         rows = pl.ds(k * rb, rb)
@@ -80,7 +85,7 @@
         cols = pl.ds(pl.multiple_of(k * 256, 256), 256)
         if half is None:
             return wdr.at[s, dev, :, cols]
-        return wdr.at[s, dev, pl.ds(64 * half, 64), cols]
+        return wdr.at[s, dev, pl.ds(pl.multiple_of(LANES // 2 * half, LANES // 2), LANES // 2), cols]
 
     streams = (
         (has_gu, gu_view, ag_send, ag_recv, lambda x: lax.rem(gidx(x), SLOTS)),
@@ -111,93 +116,78 @@
     def stash(chunk):
         return pltpu.make_async_copy(wdr.at[chunk], wd0_ref.at[chunk], sem_stash)
 
-    def ag_copies(view, send, recv, s, x):
-        def cp(name_s, name_r, dev, to, half=None):
-            v = view(x, dev, half)
-            return remote(v, v, send.at[name_s, s], recv.at[name_r, s], to)
-        return dict(
-            own_r=lambda: cp(0, 0, me, right), own_l=lambda: cp(1, 1, me, left), own_p=lambda: cp(2, 2, me, partner),
-            l_p=lambda: cp(3, 3, left, partner), l_r=lambda: cp(4, 4, left, right, 0),
-            r_p=lambda: cp(5, 5, right, partner), r_l=lambda: cp(6, 6, right, left, 1),
-            o_p=lambda: cp(7, 7, opp, partner),
-        )
-
-    def got(view, recv, send, s, x, name, dev, half=None):
-        v = view(x, dev, half)
-        remote(v, v, send.at[name, s], recv.at[name, s], partner).wait_recv()
-
     def other(dev):
         return dev + 1 - 2 * lax.rem(dev, 2)
 
+    def ag_copy(stream, x, kind):
+        _, view, send, recv, sl = stream
+        dev, half, to = (
+            (me, None, weak), (me, h, strong), (me, None, partner),
+            (weak, h, strong), (strong, h, peer), (strong, None, partner),
+            (opp, h, peer), (weak, None, partner), (opp, None, partner),
+        )[kind]
+        v = view(x, dev, half)
+        return remote(v, v, send.at[kind, sl(x)], recv.at[kind, sl(x)], to)
+
+    def got(stream, x, kind):
+        _, view, send, recv, sl = stream
+        dev, half = (
+            (strong, None), (weak, h), (partner, None),
+            (opp, h), (weak, 1 - h), (other(strong), None),
+            (opp, 1 - h), (other(weak), None), (other(opp), None),
+        )[kind]
+        v = view(x, dev, half)
+        remote(v, v, send.at[kind, sl(x)], recv.at[kind, sl(x)], partner).wait_recv()
+
+    def ag_stage(x, arrivals, sends):
+        for stream in streams:
+            @when(stream[0](x))
+            def _():
+                for kind in arrivals:
+                    got(stream, x, kind)
+                for kind in sends:
+                    ag_copy(stream, x, kind).start()
+
     def ag_step(t):
-        @when(has_gu(t + 4))
-        def _():
-            for cp in own_gu(t + 4):
+        load, start = t + 5, t + 4
+        @when(has_gu(load))
+        def _():
+            for cp in own_gu(load):
                 cp.start()
-
-        x4 = t + 4
-        @when(has_d(x4) & (lax.rem(x4, 4) == 0) & (x4 >= tiles))
-        def _():
-            own_d(x4 // 4).start()
-
-        for has, view, send, recv, sl in streams:
-            x = t + 3
-            @when(has(x))
+        @when(has_d(load) & (lax.rem(load, 4) == 0) & (load >= tiles))
+        def _():
+            own_d(load // 4).start()
+        @when(has_gu(start))
+        def _():
+            own_gu_wait(start)
+        @when(has_d(start) & (lax.rem(start, 4) == 0))
+        def _():
+            own_d(start // 4).wait()
+        ag_stage(start, (), (0, 1, 2))
+        ag_stage(t + 3, (0, 1), (3, 4, 5))
+        ag_stage(t + 2, (3, 4), (6, 7))
+        ag_stage(t + 1, (6,), (8,))
+        ag_stage(t, (2, 5, 7, 8), ())
+        for stream in streams:
+            @when(stream[0](t))
             def _():
-                if view is gu_view:
-                    own_gu_wait(x)
-                else:
-                    @when(lax.rem(x, 4) == 0)
-                    def _():
-                        own_d(x // 4).wait()
-                k = ag_copies(view, send, recv, sl(x), x)
-                k["own_r"]().start()
-                k["own_l"]().start()
-                k["own_p"]().start()
-        for has, view, send, recv, sl in streams:
-            y = t + 2
-            @when(has(y))
-            def _():
-                s = sl(y)
-                k = ag_copies(view, send, recv, s, y)
-                got(view, recv, send, s, y, 0, left)
-                k["l_r"]().start()
-                k["l_p"]().start()
-                got(view, recv, send, s, y, 1, right)
-                k["r_l"]().start()
-                k["r_p"]().start()
-        for has, view, send, recv, sl in streams:
-            z = t + 1
-            @when(has(z))
-            def _():
-                s = sl(z)
-                got(view, recv, send, s, z, 4, opp, 0)
-                got(view, recv, send, s, z, 6, opp, 1)
-                ag_copies(view, send, recv, s, z)["o_p"]().start()
-        for has, view, send, recv, sl in streams:
-            @when(has(t))
-            def _():
-                s = sl(t)
-                got(view, recv, send, s, t, 2, partner)
-                got(view, recv, send, s, t, 3, other(left))
-                got(view, recv, send, s, t, 5, other(right))
-                got(view, recv, send, s, t, 7, other(opp))
-                for make in ag_copies(view, send, recv, s, t).values():
-                    make().wait_send()
-
-    steps = 2 * tiles + 4
-    half_d, full_d, full_gu = LANES, 2 * LANES, 4 * LANES
+                for kind in range(9):
+                    ag_copy(stream, t, kind).wait_send()
+
+    steps = 2 * tiles + 2
+    full_d, full_gu = 2 * LANES, 4 * LANES
+    packet = full_d + full_gu
 
     def has_rs_gu(r):
-        return ((r >= 0) & (r < tiles)) | ((r >= tiles + 4) & (r < steps))
+        return (r >= 0) & (r < steps)
 
     def has_rs_d(r):
-        return (r >= 4) & (r < steps)
+        return ((r >= 4) & (r < tiles)) | ((r >= tiles + 2) & (r < steps))
 
     parts = ((has_rs_gu, 0, 0, full_gu), (has_rs_d, 1, full_gu, full_d))
 
     def total(r, j, rows):
-        return own[lax.rem(r, 4), c, j, rows].astype(F32) + prt[lax.rem(r, 5), j, rows].astype(F32)
+        return own[lax.rem(r, 4), j, rows].astype(F32) + prt[lax.rem(r, 5), j, rows].astype(F32)
 
     def blocks(lo, first, count, body):
         loop(first, first + count, lambda b: body(pl.ds(pl.multiple_of(lo + b * LANES, LANES), LANES)))
@@ -206,13 +196,14 @@
         _, w, lo, size = part
         s = lax.rem(r, 5)
         rows = pl.ds(lo, size)
-        return remote(own.at[lax.rem(r, 4), 1 - c, :, rows], prt.at[s, :, rows], r0_send.at[w, s], r0_recv.at[w, s], partner)
+        return remote(own.at[4 + lax.rem(r, 2), :, rows], prt.at[s, :, rows], r0_send.at[w, s], r0_recv.at[w, s], partner)
 
     def rs_far(part, r, side):
         _, w, lo, size = part
         s = lax.rem(r, 2)
         rows = pl.ds(lo + side * (size // 2), size // 2)
-        return remote(st1.at[s, rows], r1.at[s, rows], r1_send.at[w, side, s], r1_recv.at[w, side, s], (right, left)[side])
+        src = pbuf.at[pl.ds(pl.multiple_of(s * packet + lo + side * (size // 2), LANES), size // 2), 3 * TILE : 3 * TILE + LANES]
+        return remote(src, r1.at[s, rows], r1_send.at[w, side, s], r1_recv.at[w, side, s], (right, left)[side])
 
     def rs_near(part, r, side):
         _, w, lo, size = part
@@ -223,8 +214,16 @@
     def out_copy(part, r):
         _, w, lo, size = part
         s = lax.rem(r, 2)
-        to = gg_ref.at[jnp.where(r < tiles, r, r - 4)] if w == 0 else gd_ref.at[r - 4]
-        return pltpu.make_async_copy(gout.at[s, pl.ds(lo, size)], to, sem_out.at[w, s])
+        place = jnp.where(r < tiles, r, r - 2)
+        if w == 0:
+            return pltpu.make_async_copy(gout.at[s, pl.ds(lo, size)], gg_ref.at[place], sem_out.at[w, s])
+        place = jnp.where(r < tiles, r - 4, r - 2)
+        return pltpu.make_async_copy(gout.at[s, pl.ds(lo, size)], gd_ref.at[pl.ds(pl.multiple_of(place * size, size), size)], sem_out.at[w, s])
+
+    def out_copy_last_chunk(r):
+        s = lax.rem(r, 2)
+        to = gd_ref.at[pl.ds(pl.multiple_of((r - tiles + 4) * full_gu, full_gu), full_gu)]
+        return pltpu.make_async_copy(gout.at[s, pl.ds(0, full_gu)], to, sem_out.at[0, s])
 
     def rs_serve(t):
         for part in parts:
@@ -237,7 +236,7 @@
                 rs_near(part, r, 1).wait()
                 @when(r >= 4 * w + 2)
                 def _():
-                    out_copy(part, r).wait()
+                    out_copy(part, steps - 2 + s2).wait()
                 def body(rows):
                     g = total(r, i, rows) + r2[s, 0, rows].astype(F32) + r2[s, 1, rows].astype(F32)
                     g = g.astype(BF16)
@@ -245,7 +244,16 @@
                     g = g.astype(F32)
                     sq[...] += jnp.sum((g * g).reshape(LANES // 8, 8, LANES), axis=0)
                 blocks(lo, 0, size // LANES, body)
-                out_copy(part, r).start()
+                if w == 0:
+                    between_layers = (r >= tiles) & (r < tiles + 2)
+                    @when(between_layers)
+                    def _():
+                        out_copy_last_chunk(r).start()
+                    @when(jnp.logical_not(between_layers))
+                    def _():
+                        out_copy(part, r).start()
+                else:
+                    out_copy(part, r).start()
         for part in parts:
             has, _, lo, size = part
             r = t - 2
@@ -270,27 +278,32 @@
             def _():
                 s2 = lax.rem(r, 2)
                 rs_cores(part, r).wait()
-                def body(rows):
-                    st1[s2, rows] = total(r, io, rows).astype(BF16)
-                blocks(lo, 0, size // LANES, body)
+                def body(b):
+                    rows = pl.ds(pl.multiple_of(lo + b * LANES, LANES), LANES)
+                    to = pl.ds(pl.multiple_of(s2 * packet + lo + b * LANES, LANES), LANES)
+                    pbuf[to, 3 * TILE : 3 * TILE + LANES] = total(r, io, rows).astype(BF16)
+                loop(0, size // LANES, body)
                 rs_far(part, r, 0).start()
                 rs_far(part, r, 1).start()
 
     def rs_begin(r):
-        @when(has_rs_gu(r))
-        def _():
-            rs_cores(parts[0], r).start()
-        @when(has_rs_d(r))
-        def _():
-            @when(r < tiles + 4)
+        @when(has_rs_d(r) & (r < tiles))
+        def _():
+            k, cs = lax.rem(r, 4), lax.rem(r // 4 - 1, 2)
+            def body(dev):
+                cc, j = dev // chips, lax.rem(dev, chips)
+                own[place(r, cc), j, pl.ds(full_gu, full_d)] = dto[cs, cc, j, pl.ds(pl.multiple_of(k * full_d, full_d), full_d)]
+            loop(0, n, body)
+        for part in parts:
+            @when(part[0](r))
             def _():
-                s, k = lax.rem(r, 4), lax.rem(r, 4)
-                cs = lax.rem(r // 4 - 1, 2)
-                def body(dev):
-                    cc, j = dev // chips, lax.rem(dev, chips)
-                    own[s, cc, j, pl.ds(full_gu, full_d)] = dto[cs, cc, j, pl.ds(pl.multiple_of(k * full_d, full_d), full_d)]
-                loop(0, n, body)
-            rs_cores(parts[1], r).start()
+                rs_cores(part, r).start()
+
+    def last_chunk(k):
+        def body(dev):
+            cc, j = dev // chips, lax.rem(dev, chips)
+            own[place(tiles + k, cc), j, pl.ds(0, full_gu)] = dto[0, cc, j, pl.ds(pl.multiple_of(k * full_gu, full_gu), full_gu)]
+        loop(0, n, body)
 
     def back(g, u, dp):
         sig = 0.5 * jnp.tanh(0.5 * g) + 0.5
@@ -304,15 +317,18 @@
     def down_tile(s, q):
         return wdr[s, pl.ds(2 * q, 2)].reshape(TILE, d)
 
+    def place(r, cc):
+        return jnp.where(cc == c, lax.rem(r, 4), 4 + lax.rem(r, 2))
+
     def gate_up_grads(r):
-        s, m = lax.rem(r, 4), d // 2
+        m = d // 2
         def body(k):
             val = dot(at[pl.ds(pl.multiple_of(k * m, m), m)], pbuf[:, TILE : 3 * TILE]).astype(BF16)
             for e in range(m // TILE):
                 for cc in range(2):
                     lo = TILE * e + LANES * cc
                     for b in range(4):
-                        own[s, cc, 2 * k + e, LANES * b : LANES * b + LANES] = val[lo : lo + LANES, LANES * b : LANES * b + LANES]
+                        own[place(r, cc), 2 * k + e, LANES * b : LANES * b + LANES] = val[lo : lo + LANES, LANES * b : LANES * b + LANES]
         loop(0, 2, body)
 
     def down_grads_one(t):
@@ -325,10 +341,9 @@
         loop(0, 2, body)
 
     def down_grads_zero(t, r):
-        s = lax.rem(r, 4)
         val = dot(dyt[pl.ds(pl.multiple_of(lax.rem(t, 4) * TILE, TILE), TILE)], a[...]).astype(BF16)
         for dev in range(n):
-            own[s, dev % 2, dev // 2, full_gu:] = val[:, LANES * dev : LANES * dev + LANES]
+            own[place(r, dev % 2), dev // 2, full_gu:] = val[:, LANES * dev : LANES * dev + LANES]
 
     def norm_rows(h):
         wide = h.astype(F32)
@@ -338,11 +353,13 @@
     barrier = pltpu.get_barrier_semaphore()
     for k in range(1, n):
         pl.semaphore_signal(barrier, inc=1, device_id={"dp": lax.rem(me + k, n)}, device_id_type=MESH)
+    pl.semaphore_signal(barrier, inc=1, device_id=peer, device_id_type=MESH)
     for k in range(3):
         own_d(k).start()
     sq[...] = jnp.zeros_like(sq)
-    pl.semaphore_wait(barrier, n - 1)
-
+    pl.semaphore_wait(barrier, n)
+
+    ag_step(-5)
     def prologue(k):
         ag_step(k - 4)
         in_copy(k, 0).wait()
@@ -454,7 +471,7 @@
 
     def h_in(k):
         rows = pl.ds(pl.multiple_of(k * rb, rb), rb)
-        return pltpu.make_async_copy(h1_ref.at[rows], pbuf.at[rows], sem_in.at[1, k])
+        return pltpu.make_async_copy(h1_ref.at[rows], a.at[rows], sem_in.at[1, k])
 
     for k in range(4):
         h_in(k).start()
@@ -464,13 +481,16 @@
     wd0_in.start()
 
     def turn(k):
-        rs_serve(tiles + k)
-        rs_begin(tiles + k)
+        @when(lax.rem(k, 2) == 0)
+        def _():
+            rs_serve(tiles + k // 2)
+            last_chunk(k // 2)
+            rs_begin(tiles + k // 2)
         h_in(k).wait()
         def part(e):
             rows = pl.ds(pl.multiple_of(k * rb + e * LANES, LANES), LANES)
             da = acc[rows].astype(BF16).astype(F32)
-            wide = pbuf[rows].astype(F32)
+            wide = a[rows].astype(F32)
             scale = lax.rsqrt(jnp.mean(wide * wide, -1, keepdims=True) + 1e-6)
             by_scale = jnp.sum(da * wide, -1, keepdims=True)
             by_h = (da * scale - wide * (scale * scale * scale * by_scale * (1 / d))).astype(BF16)
@@ -514,7 +534,7 @@
             pbuf[rows, TILE : 2 * TILE] = dg
             pbuf[rows, 2 * TILE : 3 * TILE] = du
         loop(0, tokens // mb, rows_of)
-        r = tiles + 4 + t
+        r = tiles + 2 + t
         rs_serve(r)
         @when(q == 0)
         def _():
@@ -548,8 +568,8 @@
     return pl.pallas_call(
         functools.partial(step_kernel, n=n),
         out_shape=(
-            jax.ShapeDtypeStruct((2 * tiles, 512, LANES), BF16),
-            jax.ShapeDtypeStruct((2 * tiles, 256, LANES), BF16),
+            jax.ShapeDtypeStruct((2 * tiles, 4 * LANES, LANES), BF16),
+            jax.ShapeDtypeStruct((4 * tiles * LANES, LANES), BF16),
             jax.ShapeDtypeStruct((8, LANES), F32),
             jax.ShapeDtypeStruct((tiles, 2, tokens, TILE), F32),
             jax.ShapeDtypeStruct((3, tokens, tiles // 3 * TILE), BF16),
@@ -563,11 +583,11 @@
             v((tokens, d), BF16), v((d, tokens), BF16), v((tokens, d), BF16), v((d, tokens), BF16),
             v((tokens, d), F32), v((tokens, d), BF16),
             v((SLOTS, n, 4, LANES, LANES), BF16), v((3, n, LANES, d), BF16),
-            v((2, 2, n // 2, d, LANES), BF16), v((4, 2, n // 2, 768, LANES), BF16), v((5, n // 2, 768, LANES), BF16),
-            v((2, 768, LANES), BF16), v((2, 2, 768, LANES), BF16), v((2, 768, LANES), BF16), v((4, 2, 768, LANES), BF16),
-            v((2, 768, LANES), BF16), v((2, tokens // 4, TILE), F32), v((8, LANES), F32), v((n - 1, 8, LANES), F32),
+            v((2, 2, n // 2, d, LANES), BF16), v((6, n // 2, 768, LANES), BF16), v((5, n // 2, 768, LANES), BF16),
+            v((2, 2, 768, LANES), BF16), v((2, 768, LANES), BF16), v((4, 2, 768, LANES), BF16),
+            v((2, 768, LANES), BF16), v((2, tokens // 2, TILE), F32), v((8, LANES), F32), v((n - 1, 8, LANES), F32),
             dma((2, 4)), dma(()), dma((4,)), dma((5,)), dma((2, 2)), dma((2,)), dma((3,)), dma(()),
-            dma((8, SLOTS)), dma((8, SLOTS)), dma((8, SLOTS)), dma((8, SLOTS)),
+            dma((9, SLOTS)), dma((9, SLOTS)), dma((9, SLOTS)), dma((9, SLOTS)),
             dma((2, 5)), dma((2, 5)), dma((2, 2, 2)), dma((2, 2, 2)), dma((2, 2, 4)), dma((2, 2, 4)), dma((n - 1,)), dma((n - 1,)),
         ],
         compiler_params=pltpu.CompilerParams(collective_id=0, has_side_effects=True, vmem_limit_bytes=67_000_000),

time: 439 us -> 411 us (0.936)
  Pallas kernels: 438 us -> 410 us
    pallas_call x1, Pallas kernels: 420 us -> 392 us  [run_step(): pl.pallas_call(functools.partial(step_kernel, n=n), out_shape=(jax.ShapeD...]
where the time goes in v2:
time: 411 us
  Pallas kernels  410 us (100%)
    pallas_call x1, Pallas kernels, run_step(): pl.pallas_call(functools.partial(step_kernel, n=n), out_shape=(jax.ShapeD...  392 us
    pallas_call x1, Pallas kernels, run_adamw(): pl.pallas_call(functools.partial(adamw_kernel, count), grid=(layers, part...  18.2 us

profile of v2, /device:TPU:113, one launch (start us, length us, event | category | flops | bytes accessed | tf_op | source)
XLA Modules:
  0.0 410.5 jit_solution(7740609176382507068)
XLA Ops:
  0.6 391.5 %step.1 = (bf16[24,512,128]{2,1,0:T(8,128)(2,1)}, bf16[6144,128]{1,0:T(8,128)(2,1)}, f32[8,128]{1,0:T(8,128)}, f32[12,2,2048,256]{3,2,1,0:T(8,128)}, bf16[3,2048...) custom-call(bf16[1,2048,1024]{2,1,0:T(8,128)(2,1)} %x_ref.1, ...), custom_call_target="tpu_custom_call" | custom-call | flops 193273528320 | bytes 200000000 | tf_op jit(solution)/shard_map/step/pallas_call | solution.py:568
  392.2 18.2 %adamw.1 = (bf16[2,128,3072]{2,1,0:T(8,128)(2,1)}, bf16[2,128,3072]{2,1,0:T(8,128)(2,1)}, bf16[2,384,1024]{2,1,0:T(8,128)(2,1)}, f32[2,128,3072]{2,1,0:T(8,128)}...) custom-call(f32[8,128]{1,0:T(8,128)} %get-tuple-element.12.ssq_ref, ...), custom_call_target="tpu_custom_call" | custom-call | tf_op jit(solution)/shard_map/adamw/pallas_call | solution.py:636

commit v3 on v2

--- a/solution.py
+++ b/solution.py
@@ -34,7 +34,7 @@
 def step_kernel(
     x_ref, dy_ref, wg_ref, wu_ref, wd_ref,
     gg_ref, gd_ref, ssq_ref, gu0_ref, p0_ref, h1_ref, a0t_ref, wd0_ref,
-    a, at, dyb, dyt, acc, pbuf, gsl, wdr, dto, own, prt, st2, r1, r2, gout, stg, sq, sqall,
+    a, at, dyb, dyt, acc, pbuf, gsl, wdr, dto, own, prt, st1, st2, r1, r2, gout, stg, sq, sqall,
     sem_in, sem_stg, sem_p, sem_h, sem_out, sem_own, sem_wd, sem_stash,
     ag_send, ag_recv, dg_send, dg_recv, r0_send, r0_recv, r1_send, r1_recv, r2_send, r2_recv, sq_send, sq_recv,
     *, n,
@@ -176,7 +176,6 @@
 
     steps = 2 * tiles + 2
     full_d, full_gu = 2 * LANES, 4 * LANES
-    packet = full_d + full_gu
 
     def has_rs_gu(r):
         return (r >= 0) & (r < steps)
@@ -202,8 +201,7 @@
         _, w, lo, size = part
         s = lax.rem(r, 2)
         rows = pl.ds(lo + side * (size // 2), size // 2)
-        src = pbuf.at[pl.ds(pl.multiple_of(s * packet + lo + side * (size // 2), LANES), size // 2), 3 * TILE : 3 * TILE + LANES]
-        return remote(src, r1.at[s, rows], r1_send.at[w, side, s], r1_recv.at[w, side, s], (right, left)[side])
+        return remote(st1.at[s, rows], r1.at[s, rows], r1_send.at[w, side, s], r1_recv.at[w, side, s], (right, left)[side])
 
     def rs_near(part, r, side):
         _, w, lo, size = part
@@ -278,11 +276,9 @@
             def _():
                 s2 = lax.rem(r, 2)
                 rs_cores(part, r).wait()
-                def body(b):
-                    rows = pl.ds(pl.multiple_of(lo + b * LANES, LANES), LANES)
-                    to = pl.ds(pl.multiple_of(s2 * packet + lo + b * LANES, LANES), LANES)
-                    pbuf[to, 3 * TILE : 3 * TILE + LANES] = total(r, io, rows).astype(BF16)
-                loop(0, size // LANES, body)
+                def body(rows):
+                    st1[s2, rows] = total(r, io, rows).astype(BF16)
+                blocks(lo, 0, size // LANES, body)
                 rs_far(part, r, 0).start()
                 rs_far(part, r, 1).start()
 
@@ -308,36 +304,38 @@
     def back(g, u, dp):
         sig = 0.5 * jnp.tanh(0.5 * g) + 0.5
         silu = g * sig
-        dp = dp.astype(BF16).astype(F32)
+        dp = dp.astype(F32)
         return silu, (dp * u * (sig * (1 + g * (1 - sig)))).astype(BF16), (dp * silu).astype(BF16)
 
     def gate_up(s):
         return jnp.concatenate([gsl[s, :, b].reshape(d, LANES) for b in range(4)], axis=1)
 
-    def down_tile(s, q):
-        return wdr[s, pl.ds(2 * q, 2)].reshape(TILE, d)
+    def dp_pair(ch, q):
+        def rows_of(m):
+            rows = pl.ds(pl.multiple_of(m * mb, mb), mb)
+            val = dot_nt(dyb[rows], wdr[ch, pl.ds(2 * q, 4)].reshape(2 * TILE, d)).astype(BF16)
+            pbuf[rows, :TILE] = val[:, :TILE]
+            pbuf[rows, 3 * TILE :] = val[:, TILE:]
+        loop(0, tokens // mb, rows_of)
 
     def place(r, cc):
         return jnp.where(cc == c, lax.rem(r, 4), 4 + lax.rem(r, 2))
 
-    def gate_up_grads(r):
+    def weight_grads(r, t=None):
         m = d // 2
         def body(k):
-            val = dot(at[pl.ds(pl.multiple_of(k * m, m), m)], pbuf[:, TILE : 3 * TILE]).astype(BF16)
+            rows = pl.ds(pl.multiple_of(k * m, m), m)
+            val = dot(at[rows], pbuf[:, TILE : 3 * TILE]).astype(BF16)
+            if t is not None:
+                cs, q = lax.rem(t // 4, 2), lax.rem(t, 4)
+                more = dot(dyt[rows], pbuf[:, :TILE]).astype(BF16)
+                for cc in range(2):
+                    dto[cs, cc, q, rows] = more[:, LANES * cc : LANES * cc + LANES]
             for e in range(m // TILE):
                 for cc in range(2):
                     lo = TILE * e + LANES * cc
                     for b in range(4):
                         own[place(r, cc), 2 * k + e, LANES * b : LANES * b + LANES] = val[lo : lo + LANES, LANES * b : LANES * b + LANES]
-        loop(0, 2, body)
-
-    def down_grads_one(t):
-        cs, q, m = lax.rem(t // 4, 2), lax.rem(t, 4), d // 2
-        def body(k):
-            rows = pl.ds(pl.multiple_of(k * m, m), m)
-            val = dot(dyt[rows], pbuf[:, :TILE]).astype(BF16)
-            for cc in range(2):
-                dto[cs, cc, q, rows] = val[:, LANES * cc : LANES * cc + LANES]
         loop(0, 2, body)
 
     def down_grads_zero(t, r):
@@ -374,8 +372,8 @@
     a0t_copy = pltpu.make_async_copy(at, a0t_ref, sem_h.at[0])
     a0t_copy.start()
 
-    def stg_copy(t, m):
-        return pltpu.make_async_copy(stg, gu0_ref.at[t, :, pl.ds(pl.multiple_of(m * mf, mf), mf)], sem_stg)
+    def stg_copy(slot, t, row):
+        return pltpu.make_async_copy(stg.at[slot], gu0_ref.at[t, :, pl.ds(pl.multiple_of(row, TILE), TILE)], sem_stg.at[slot])
 
     def p_copy(t):
         q = lax.rem(t, 4)
@@ -396,12 +394,15 @@
             rows = pl.ds(pl.multiple_of(m * mf, mf), mf)
             val = dot(a[rows], gate_up(s))
             g, u = val[:, :TILE], val[:, TILE:]
-            @when((m > 0) | (t > 0))
-            def _():
-                stg_copy(t, m).wait()
-            stg[0] = g
-            stg[1] = u
-            stg_copy(t, m).start()
+            for e in range(mf // TILE):
+                turn_no = t * (tokens // TILE) + m * (mf // TILE) + e
+                slot = lax.rem(turn_no, 3)
+                @when(turn_no >= 3)
+                def _():
+                    stg_copy(slot, 0, 0).wait()
+                stg[slot, 0] = g[TILE * e : TILE * e + TILE]
+                stg[slot, 1] = u[TILE * e : TILE * e + TILE]
+                stg_copy(slot, t, m * mf + TILE * e).start()
             sig = 0.5 * jnp.tanh(0.5 * g) + 0.5
             pbuf[rows, pl.ds(pl.multiple_of(q * TILE, TILE), TILE)] = (g * sig * u).astype(BF16)
         loop(0, tokens // mf, rows_of)
@@ -414,7 +415,8 @@
                 acc[rows] += dot(pbuf[rows], wdr[ch].reshape(d, d))
             loop(0, tokens // mf, down)
     loop(0, tiles, forward)
-    stg_copy(0, 0).wait()
+    for slot in range(3):
+        stg_copy(slot, 0, 0).wait()
     for q in range(4):
         p_copy(q).wait()
     a0t_copy.wait()
@@ -452,20 +454,22 @@
         ag_step(tiles + 4 + t)
         q, ch = lax.rem(t, 4), t // 4
         s = lax.rem(tiles + t, SLOTS)
+        @when(lax.rem(q, 2) == 0)
+        def _():
+            dp_pair(ch, q)
+        dp_at = pl.multiple_of(3 * TILE * lax.rem(q, 2), TILE)
         def rows_of(m):
             rows = pl.ds(pl.multiple_of(m * mb, mb), mb)
             val = dot(a[rows], gate_up(s))
             g, u = val[:, :TILE], val[:, TILE:]
-            dp = dot_nt(dyb[rows], down_tile(ch, q))
-            silu, dg, du = back(g, u, dp)
+            silu, dg, du = back(g, u, pbuf[rows, pl.ds(dp_at, TILE)])
             pbuf[rows, :TILE] = (silu * u).astype(BF16)
             pbuf[rows, TILE : 2 * TILE] = dg
             pbuf[rows, 2 * TILE : 3 * TILE] = du
             acc[rows] += dot_nt(jnp.concatenate([dg, du], axis=1), gate_up(s))
         loop(0, tokens // mb, rows_of)
         rs_serve(t)
-        gate_up_grads(t)
-        down_grads_one(t)
+        weight_grads(t, t)
         rs_begin(t)
     loop(0, tiles, layer_one)
 
@@ -527,7 +531,7 @@
         base = pl.multiple_of(2 * TILE * lax.rem(t, 2), 2 * TILE)
         def rows_of(m):
             rows = pl.ds(pl.multiple_of(m * mb, mb), mb)
-            dp = dot_nt(dyb[rows], down_tile(ch, q))
+            dp = dot_nt(dyb[rows], wdr[ch, pl.ds(2 * q, 2)].reshape(TILE, d)).astype(BF16)
             g = acc[rows, pl.ds(base, TILE)]
             u = acc[rows, pl.ds(pl.multiple_of(base + TILE, TILE), TILE)]
             _, dg, du = back(g, u, dp)
@@ -539,7 +543,7 @@
         @when(q == 0)
         def _():
             p_in(ch).wait()
-        gate_up_grads(r)
+        weight_grads(r)
         down_grads_zero(t, r)
         rs_begin(r)
     loop(0, tiles, layer_zero)
@@ -584,9 +588,9 @@
             v((tokens, d), F32), v((tokens, d), BF16),
             v((SLOTS, n, 4, LANES, LANES), BF16), v((3, n, LANES, d), BF16),
             v((2, 2, n // 2, d, LANES), BF16), v((6, n // 2, 768, LANES), BF16), v((5, n // 2, 768, LANES), BF16),
-            v((2, 2, 768, LANES), BF16), v((2, 768, LANES), BF16), v((4, 2, 768, LANES), BF16),
-            v((2, 768, LANES), BF16), v((2, tokens // 2, TILE), F32), v((8, LANES), F32), v((n - 1, 8, LANES), F32),
-            dma((2, 4)), dma(()), dma((4,)), dma((5,)), dma((2, 2)), dma((2,)), dma((3,)), dma(()),
+            v((2, 768, LANES), BF16), v((2, 2, 768, LANES), BF16), v((2, 768, LANES), BF16), v((4, 2, 768, LANES), BF16),
+            v((2, 768, LANES), BF16), v((3, 2, TILE, TILE), F32), v((8, LANES), F32), v((n - 1, 8, LANES), F32),
+            dma((2, 4)), dma((3,)), dma((4,)), dma((5,)), dma((2, 2)), dma((2,)), dma((3,)), dma(()),
             dma((9, SLOTS)), dma((9, SLOTS)), dma((9, SLOTS)), dma((9, SLOTS)),
             dma((2, 5)), dma((2, 5)), dma((2, 2, 2)), dma((2, 2, 2)), dma((2, 2, 4)), dma((2, 2, 4)), dma((n - 1,)), dma((n - 1,)),
         ],

time: 411 us -> 405 us (0.985)
  Pallas kernels: 410 us -> 404 us
    pallas_call x1, Pallas kernels: 392 us -> 386 us  [run_step(): pl.pallas_call(functools.partial(step_kernel, n=n), out_shape=(jax.ShapeD...]
where the time goes in v3:
time: 405 us
  Pallas kernels  404 us (100%)
    pallas_call x1, Pallas kernels, run_step(): pl.pallas_call(functools.partial(step_kernel, n=n), out_shape=(jax.ShapeD...  386 us
    pallas_call x1, Pallas kernels, run_adamw(): pl.pallas_call(functools.partial(adamw_kernel, count), grid=(layers, part...  18.2 us

profile of v3, /device:TPU:113, one launch (start us, length us, event | category | flops | bytes accessed | tf_op | source)
XLA Modules:
  0.0 405.1 jit_solution(2747636290224521088)
XLA Ops:
  0.6 386.1 %step.1 = (bf16[24,512,128]{2,1,0:T(8,128)(2,1)}, bf16[6144,128]{1,0:T(8,128)(2,1)}, f32[8,128]{1,0:T(8,128)}, f32[12,2,2048,256]{3,2,1,0:T(8,128)}, bf16[3,2048...) custom-call(bf16[1,2048,1024]{2,1,0:T(8,128)(2,1)} %x_ref.1, ...), custom_call_target="tpu_custom_call" | custom-call | flops 193273528320 | bytes 200000000 | tf_op jit(solution)/shard_map/step/pallas_call | solution.py:572
  386.7 18.2 %adamw.1 = (bf16[2,128,3072]{2,1,0:T(8,128)(2,1)}, bf16[2,128,3072]{2,1,0:T(8,128)(2,1)}, bf16[2,384,1024]{2,1,0:T(8,128)(2,1)}, f32[2,128,3072]{2,1,0:T(8,128)}...) custom-call(f32[8,128]{1,0:T(8,128)} %get-tuple-element.12.ssq_ref, ...), custom_call_target="tpu_custom_call" | custom-call | tf_op jit(solution)/shard_map/adamw/pallas_call | solution.py:640
